TPU v7x, 32 devices: a whole 2x2x4 slice. The times are simulated.
32 devices in a mesh: groups: 2 (over y), wide: 8 (over z, x), narrow: 2 (over core).
Axes of the slice: x: 2, y: 2, z: 4, core: 2. Of those that a mesh axis runs over, the one named last changes fastest.
Arguments:
- queries: bfloat16 [4, 2048, 64], P(('groups', 'narrow'), 'wide'), parts along dimension 0, may hold values from -6 to 6
- key_rows: bfloat16 [4, 2048, 64], P(('groups', 'narrow'), 'wide'), parts along dimension 0, may hold values from -6 to 6
- values: bfloat16 [4, 2048, 64], P(('groups', 'narrow'), 'wide'), parts along dimension 0, may hold values from -6 to 6
- log_gate: float32 [4, 2048], P(('groups', 'narrow'), 'wide'), parts along dimension 0, may hold values from -0.8 to 0, as said below
- lengths: int32 [4], P(('groups', 'narrow')), parts along dimension 0, may hold values from 1024 to 2048
- cont_queries: bfloat16 [160, 64], P(('groups', 'wide', 'narrow')), parts along dimension 0, may hold values from -6 to 6
- cont_prompt: int32 [160], P(('groups', 'wide', 'narrow')), parts along dimension 0, may hold values from 0 to 1
Outputs:
- prompt_out: bfloat16 [4, 2048, 64], P(('groups', 'narrow'), 'wide'), parts along dimension 0
- cont_out: bfloat16 [160, 64], P(('groups', 'wide', 'narrow')), parts along dimension 0
There are 2 independent parts, one for each index of `groups`. A program takes and returns all parts, laid end to end along the dimension named above; each array names one. Nothing has to cross between parts.
Inputs may be any that keep to these rules, and one draw needn't show every extreme that they name: `log_gate`: gates only shrink the state: every entry is at most zero.
All inputs are finite; a program needn't handle non-finite values.
Results may differ from a plain program's by a relative error of at most 0.0067.
Values may be sent and summed in bfloat16 or wider, within the bound.
No kernel may reach another device: no remote copies, remote signals or barrier semaphores. Data moves between devices by JAX's collectives and lax.ppermute only.
A program may use at most 64 MiB of HBM per device.

v0:
```python
import jax
import jax.numpy as jnp
import numpy as np
from jax import lax
from jax.sharding import PartitionSpec as P

epsilon = 1e-06
block_rows = 1024


def rms_rows(running):
    return running * lax.rsqrt(jnp.mean(running * running, axis=-1, keepdims=True) + epsilon)


def extend_zeros(table, pad_count):
    return np.concatenate([table, np.zeros((pad_count,), table.dtype)])


def pair_tables(head_width, shard_count):
    lead_index, trail_index = np.triu_indices(head_width)
    doubled = np.where(lead_index == trail_index, 1.0, 2.0)
    feature_count = lead_index.shape[0]
    padded_rows = -(-feature_count // shard_count) * shard_count
    block_width = min(block_rows, padded_rows)
    full_length = -(-padded_rows // block_width) * block_width
    pad_count = full_length - lead_index.shape[0]
    lead_index = extend_zeros(lead_index, pad_count).astype(np.int32)
    trail_index = extend_zeros(trail_index, pad_count).astype(np.int32)
    doubled = extend_zeros(doubled, pad_count).astype(np.float32)
    live_pairs = (doubled > 0).astype(np.float32)
    return (
        jnp.asarray(lead_index),
        jnp.asarray(trail_index),
        jnp.asarray(doubled),
        jnp.asarray(live_pairs),
        padded_rows,
        block_width,
        full_length,
    )


def pair_block(rows, lead_part, trail_part, forget_multiplier):
    leading_columns = jnp.take(rows, lead_part, axis=1).astype(jnp.float32)
    right_cols = jnp.take(rows, trail_part, axis=1).astype(jnp.float32)
    return (leading_columns * right_cols * forget_multiplier[None, :]).astype(jnp.bfloat16)


def block_state(key_rows, spread, tables):
    lead_all, trail_all, doubled_all, live_pairs, padded_rows, block_width, full_length = tables
    head_width = key_rows.shape[1]

    def fill_block(block_index, state):
        first_row = block_index * block_width
        features = pair_block(
            key_rows,
            lax.dynamic_slice_in_dim(lead_all, first_row, block_width),
            lax.dynamic_slice_in_dim(trail_all, first_row, block_width),
            lax.dynamic_slice_in_dim(live_pairs, first_row, block_width),
        )
        state_block = lax.dot_general(
            features, spread, (((0,), (0,)), ((), ())), preferred_element_type=jnp.float32
        )
        return lax.dynamic_update_slice_in_dim(
            state, state_block.astype(jnp.bfloat16), first_row, 0
        )

    initial = jnp.zeros((full_length, head_width), jnp.bfloat16)
    return lax.fori_loop(0, full_length // block_width, fill_block, initial)[:padded_rows]


def carried_read(query_rows, carried, tables):
    lead_all, trail_all, doubled_all, live_pairs, padded_rows, block_width, full_length = tables
    row_count, head_width = query_rows.shape
    if full_length > padded_rows:
        carried = jnp.pad(carried, ((0, full_length - padded_rows), (0, 0)))

    def add_block(block_index, running):
        first_row = block_index * block_width
        features = pair_block(
            query_rows,
            lax.dynamic_slice_in_dim(lead_all, first_row, block_width),
            lax.dynamic_slice_in_dim(trail_all, first_row, block_width),
            lax.dynamic_slice_in_dim(doubled_all, first_row, block_width),
        )
        state_rows = lax.dynamic_slice_in_dim(carried, first_row, block_width, 0)
        return running + jnp.dot(features, state_rows, preferred_element_type=jnp.float32)

    return lax.fori_loop(
        0, full_length // block_width, add_block, jnp.zeros((row_count, head_width), jnp.float32)
    )


def owner_prefix(sent_slices, totals):
    shard_count = totals.shape[0]
    inclusive = jnp.cumsum(totals)
    exclusive = jnp.concatenate([jnp.zeros((1,), jnp.float32), inclusive])
    target = lax.iota(jnp.int32, shard_count + 1)[:, None]
    source = lax.iota(jnp.int32, shard_count)[None, :]
    weight = jnp.exp(jnp.where(source < target, exclusive[:, None] - inclusive[None, :], -jnp.inf))
    return jnp.einsum(
        "wu,urn->wrn", weight, sent_slices.astype(jnp.float32), precision=lax.Precision.HIGHEST
    )


def prompt_rows(query_rows, key_rows, payload_lines, cumulative, live_mask, carried, tables):
    row_count, head_width = query_rows.shape
    scores = lax.dot_general(
        query_rows, key_rows, (((1,), (1,)), ((), ())), preferred_element_type=jnp.float32
    )
    row_ids = lax.iota(jnp.int32, row_count)
    lower_mask = row_ids[:, None] >= row_ids[None, :]
    decay_matrix = jnp.exp(
        jnp.where(lower_mask, cumulative[:, None] - cumulative[None, :], -jnp.inf)
    )
    weights = (scores * scores * decay_matrix * live_mask[None, :]).astype(jnp.bfloat16)
    local_term = jnp.dot(weights, payload_lines, preferred_element_type=jnp.float32)
    carried_term = carried_read(query_rows, carried, tables)
    running = local_term + jnp.exp(cumulative)[:, None] * carried_term
    return (live_mask[:, None] * rms_rows(running)).astype(jnp.bfloat16)


def on_device(queries, key_rows, values, log_gate, lengths, cont_queries, cont_prompt):
    wide_count = lax.axis_size("wide")
    lane_count = lax.axis_size("narrow")
    owner_index = lax.axis_index("wide")
    prompt_lane = lax.axis_index("narrow")
    query_rows = queries[0]
    own_keys = key_rows[0]
    payload_lines = values[0]
    row_count, head_width = own_keys.shape
    tables = pair_tables(head_width, wide_count)
    lead_all, trail_all, doubled_all = (tables[0], tables[1], tables[2])
    padded_rows = tables[4]
    rows_per = padded_rows // wide_count
    position = owner_index * row_count + lax.iota(jnp.int32, row_count)
    live_mask = (position < lengths[0]).astype(jnp.float32)
    cumulative = jnp.cumsum(log_gate[0] * live_mask)
    piece_number = cumulative[-1]
    scaled = live_mask * jnp.exp(piece_number - cumulative)
    spread = (scaled[:, None] * payload_lines.astype(jnp.float32)).astype(jnp.bfloat16)
    span_state = block_state(own_keys, spread, tables)
    totals = lax.all_gather(piece_number[None], "wide", axis=0, tiled=True)
    sent_slices = lax.all_to_all(
        span_state.reshape(wide_count, rows_per, head_width),
        "wide",
        split_axis=0,
        concat_axis=0,
        tiled=True,
    )
    rounded = owner_prefix(sent_slices, totals).astype(jnp.bfloat16)
    carried_slices = lax.all_to_all(
        rounded[:wide_count], "wide", split_axis=0, concat_axis=0, tiled=True
    )
    carried = carried_slices.reshape(padded_rows, head_width)
    final_slice = rounded[wide_count]
    prompt_out = prompt_rows(
        query_rows, own_keys, payload_lines, cumulative, live_mask, carried, tables
    )
    prompt_ids = lax.iota(jnp.int32, lane_count)[:, None]
    chosen = (cont_prompt[None, :] == prompt_ids)[:, :, None]
    masked = jnp.where(chosen, cont_queries[None, :, :], jnp.zeros_like(cont_queries)[None, :, :])
    pair_rows = lax.all_gather(masked, "narrow", axis=1, tiled=True)
    own_rows = lax.dynamic_index_in_dim(pair_rows, prompt_lane, 0, keepdims=False)
    initial = jnp.zeros((own_rows.shape[0], head_width), jnp.float32)
    shard_portion = lax.all_gather(final_slice, "wide", axis=0, tiled=True)
    piece_rows = shard_portion.shape[0]
    features = pair_block(
        own_rows,
        lax.slice_in_dim(lead_all, 0, piece_rows, axis=0),
        lax.slice_in_dim(trail_all, 0, piece_rows, axis=0),
        lax.slice_in_dim(doubled_all, 0, piece_rows, axis=0),
    )
    partial_value = initial + jnp.dot(features, shard_portion, preferred_element_type=jnp.float32)
    running = lax.psum_scatter(partial_value, "narrow", scatter_dimension=0, tiled=True)
    cont_out = rms_rows(running).astype(jnp.bfloat16)
    return (prompt_out[None], cont_out)


def solution(mesh):
    in_specs = (
        P(("groups", "narrow"), "wide", None),
        P(("groups", "narrow"), "wide", None),
        P(("groups", "narrow"), "wide", None),
        P(("groups", "narrow"), "wide"),
        P(("groups", "narrow")),
        P(("groups", "wide", "narrow"), None),
        P(("groups", "wide", "narrow")),
    )
    out_specs = (P(("groups", "narrow"), "wide", None), P(("groups", "wide", "narrow"), None))
    return jax.shard_map(
        on_device, mesh=mesh, in_specs=in_specs, out_specs=out_specs, check_vma=False
    )
```

profile of v0, /device:TPU:0, one launch (start us, length us, event | category | flops | bytes accessed | tf_op | source)
XLA Modules:
  0.0 162.9 jit_solution(10118833108402280067)
XLA Ops:
  2.6 0.9 copy.25
  3.5 1.2 dynamic-slice
  4.7 1.3 slice_dynamic-update-slice_fusion
  6.8 33.6 %while.29 = (s32[]{:T(128)}, bf16[3072,64]{0,1:T(8,128)(2,1)S(1)}, bf16[256,64]{0,1:T(8,128)(2,1)}, bf16[256,64]{1,0:T(8,128)(2,1)S(1)}, s32[]{:T(128)}, /*index...) while((s32[]{:T(128)}, bf16[3072,64]{0,1:T(8,128)(2,1)S(1)}, ...), condition=%wide.region_4.6_spmd.clone, body=%wide.region_3.5_spmd.sunk.clone.sunk | while | flops 35475460 | bytes 3522759 | solution.py:68
  7.5 3.9 %gather_fusion = bf16[1024,256]{1,0:T(8,128)(2,1)S(1)} fusion(bf16[256,64]{0,1:T(8,128)(2,1)S(1)} %copy-done.1, s32[1024]{0:T(1024)S(1)} %get-tuple-element.395), kind=kCustom, calls=%fused_computation.2.clone.clone.1 | custom fusion | bytes 1052672 | tf_op jit(solution)/shard_map/while/body/eval_jaxpr/jit(_take)/gather | solution.py:44
  11.5 3.9 %gather_fusion.1 = bf16[1024,256]{1,0:T(8,128)(2,1)S(1)} fusion(bf16[256,64]{0,1:T(8,128)(2,1)S(1)} %copy-done.1, s32[1024]{0:T(1024)S(1)} %get-tuple-element.396), kind=kCustom, calls=%fused_computation.clone.clone.1 | custom fusion | bytes 1052672 | tf_op jit(solution)/shard_map/while/body/eval_jaxpr/jit(_take)/gather | solution.py:43
  16.8 1.1 fusion.87
  18.8 3.9 %gather_fusion = bf16[1024,256]{1,0:T(8,128)(2,1)S(1)} fusion(bf16[256,64]{0,1:T(8,128)(2,1)S(1)} %copy-done.1, s32[1024]{0:T(1024)S(1)} %get-tuple-element.395), kind=kCustom, calls=%fused_computation.2.clone.clone.1 | custom fusion | bytes 1052672 | tf_op jit(solution)/shard_map/while/body/eval_jaxpr/jit(_take)/gather | solution.py:44
  22.7 3.9 %gather_fusion.1 = bf16[1024,256]{1,0:T(8,128)(2,1)S(1)} fusion(bf16[256,64]{0,1:T(8,128)(2,1)S(1)} %copy-done.1, s32[1024]{0:T(1024)S(1)} %get-tuple-element.396), kind=kCustom, calls=%fused_computation.clone.clone.1 | custom fusion | bytes 1052672 | tf_op jit(solution)/shard_map/while/body/eval_jaxpr/jit(_take)/gather | solution.py:43
  28.1 1.1 fusion.87
  30.0 3.9 %gather_fusion = bf16[1024,256]{1,0:T(8,128)(2,1)S(1)} fusion(bf16[256,64]{0,1:T(8,128)(2,1)S(1)} %copy-done.1, s32[1024]{0:T(1024)S(1)} %get-tuple-element.395), kind=kCustom, calls=%fused_computation.2.clone.clone.1 | custom fusion | bytes 1052672 | tf_op jit(solution)/shard_map/while/body/eval_jaxpr/jit(_take)/gather | solution.py:44
  33.9 3.9 %gather_fusion.1 = bf16[1024,256]{1,0:T(8,128)(2,1)S(1)} fusion(bf16[256,64]{0,1:T(8,128)(2,1)S(1)} %copy-done.1, s32[1024]{0:T(1024)S(1)} %get-tuple-element.396), kind=kCustom, calls=%fused_computation.clone.clone.1 | custom fusion | bytes 1052672 | tf_op jit(solution)/shard_map/while/body/eval_jaxpr/jit(_take)/gather | solution.py:43
  39.3 1.1 fusion.87
  41.0 0.8 copy.26
  41.7 7.4 %all-to-all-start = ((bf16[8,260,64]{1,2,0:T(8,128)(2,1)}), bf16[8,260,64]{1,2,0:T(8,128)(2,1)S(1)}, u32[]{:S(2)}, u32[]{:S(2)}) async-start(bf16[8,260,64]{1,2,0:T(8,128)(2,1)} %copy.26), calls=%async_computation | async-start | bytes 786432 | tf_op jit(solution)/shard_map/all_to_all | solution.py:143
  49.3 1.8 %all_gather.10 = bf16[2,10,64]{2,0,1:T(2,128)(2,1)S(1)} all-gather(bf16[2,5,64]{2,0,1:T(2,128)(2,1)S(1)} %broadcast_select_fusion), channel_id=1, replica_groups=mesh['groups'=2,'wide'=8,'narrow'=2] {'narrow'}, dimensions={1}, use_global_device_ids=true | all-gather | bytes 3840 | tf_op jit(solution)/shard_map/all_gather | solution.py:162
  51.2 21.8 %all-reduce.1 = f32[8]{0:T(128)S(1)} all-reduce(f32[8]{0:T(128)S(1)} %get-tuple-element.337), channel_id=1, replica_groups=mesh['groups'=2,'wide'=8,'narrow'=2] {'wide'}, use_global_device_ids=true, to_apply=%add.1 | all-reduce | flops 8 | bytes 64
  73.3 4.8 %gather_fusion.4 = bf16[2080,10]{1,0:T(8,128)(2,1)S(1)} fusion(bf16[10,64]{0,1:T(8,128)(2,1)S(1)} %bitcast.90, s32[3072]{0:T(1024)S(1)} %pad_clamp_fusion.1), kind=kCustom, calls=%fused_computation.1.clone | custom fusion | bytes 91520 | tf_op jit(solution)/shard_map/jit(_take)/gather | solution.py:43
  78.1 4.8 %gather_fusion.5 = bf16[2080,10]{1,0:T(8,128)(2,1)S(1)} fusion(bf16[10,64]{0,1:T(8,128)(2,1)S(1)} %bitcast.91, s32[3072]{0:T(1024)S(1)} %pad_clamp_fusion), kind=kCustom, calls=%fused_computation.5.clone | custom fusion | bytes 91520 | tf_op jit(solution)/shard_map/jit(_take)/gather | solution.py:44
  84.2 0.9 convolution_convert_fusion.1
  85.4 33.2 %all-gather = bf16[1,2080,64]{2,0,1:T(2,128)(2,1)S(1)} all-gather(bf16[1,260,64]{2,0,1:T(2,128)(2,1)S(1)} %copy.32), channel_id=2, replica_groups=mesh['groups'=2,'wide'=8,'narrow'=2] {'wide'}, dimensions={1}, use_global_device_ids=true | all-gather | bytes 299520 | tf_op jit(solution)/shard_map/all_gather | solution.py:165
  118.6 1.3 copy.33
  120.7 3.5 %all-to-all-start.1 = ((bf16[8,260,64]{1,2,0:T(8,128)(2,1)}), bf16[8,260,64]{1,2,0:T(8,128)(2,1)S(1)}, u32[]{:S(2)}, u32[]{:S(2)}) async-start(bf16[8,260,64]{1,2,0:T(8,128)(2,1)} %copy.28), calls=%async_computation.1 | async-start | bytes 786432 | tf_op jit(solution)/shard_map/all_to_all | solution.py:151
  124.8 2.5 %all-reduce.2 = f32[10,64]{1,0:T(8,128)S(1)} all-reduce(f32[10,64]{1,0:T(8,128)S(1)} %fusion.42), channel_id=3, replica_groups=mesh['groups'=2,'wide'=8,'narrow'=2] {'narrow'}, use_global_device_ids=true, to_apply=%region_8.11.clone | all-reduce | flops 640 | bytes 5120
  128.0 5.3 %all-to-all-done.1 = bf16[8,260,64]{1,2,0:T(8,128)(2,1)S(1)} async-done(((bf16[8,260,64]{1,2,0:T(8,128)(2,1)}), bf16[8,260,64]{1,2,0:T(8,128)(2,1)S(1)}, u32[]{:S(2)}, u32[]{:S(2)}) %all-to-all-start.1) | async-done | bytes 266272 | tf_op jit(solution)/shard_map/all_to_all | solution.py:151
  133.9 27.9 %while.30 = (s32[]{:T(128)}, f32[256,64]{0,1:T(8,128)S(1)}, bf16[256,64]{0,1:T(8,128)(2,1)S(1)}, bf16[3072,64]{0,1:T(8,128)(2,1)S(1)}, s32[]{:T(128)}, /*index=5...) while((s32[]{:T(128)}, f32[256,64]{0,1:T(8,128)S(1)}, ...), condition=%wide.region_6.8_spmd.clone.clone, body=%wide.region_5.7_spmd.sunk.clone.clone.sunk | while | flops 35442696 | bytes 3457205 | solution.py:88
  134.0 3.9 %gather_fusion.2 = bf16[1024,256]{1,0:T(8,128)(2,1)S(1)} fusion(bf16[256,64]{0,1:T(8,128)(2,1)S(1)} %get-tuple-element.464, s32[1024]{0:T(1024)S(1)} %get-tuple-element.403), kind=kCustom, calls=%fused_computation.4.clone.clone.1 | custom fusion | bytes 1052672 | tf_op jit(solution)/shard_map/while/body/eval_jaxpr/jit(_take)/gather | solution.py:44
  137.9 3.9 %gather_fusion.3 = bf16[1024,256]{1,0:T(8,128)(2,1)S(1)} fusion(bf16[256,64]{0,1:T(8,128)(2,1)S(1)} %get-tuple-element.464, s32[1024]{0:T(1024)S(1)} %get-tuple-element.404), kind=kCustom, calls=%fused_computation.3.clone.clone.1 | custom fusion | bytes 1052672 | tf_op jit(solution)/shard_map/while/body/eval_jaxpr/jit(_take)/gather | solution.py:43
  143.3 3.9 %gather_fusion.2 = bf16[1024,256]{1,0:T(8,128)(2,1)S(1)} fusion(bf16[256,64]{0,1:T(8,128)(2,1)S(1)} %get-tuple-element.464, s32[1024]{0:T(1024)S(1)} %get-tuple-element.403), kind=kCustom, calls=%fused_computation.4.clone.clone.1 | custom fusion | bytes 1052672 | tf_op jit(solution)/shard_map/while/body/eval_jaxpr/jit(_take)/gather | solution.py:44
  147.2 3.9 %gather_fusion.3 = bf16[1024,256]{1,0:T(8,128)(2,1)S(1)} fusion(bf16[256,64]{0,1:T(8,128)(2,1)S(1)} %get-tuple-element.464, s32[1024]{0:T(1024)S(1)} %get-tuple-element.404), kind=kCustom, calls=%fused_computation.3.clone.clone.1 | custom fusion | bytes 1052672 | tf_op jit(solution)/shard_map/while/body/eval_jaxpr/jit(_take)/gather | solution.py:43
  152.6 3.9 %gather_fusion.2 = bf16[1024,256]{1,0:T(8,128)(2,1)S(1)} fusion(bf16[256,64]{0,1:T(8,128)(2,1)S(1)} %get-tuple-element.464, s32[1024]{0:T(1024)S(1)} %get-tuple-element.403), kind=kCustom, calls=%fused_computation.4.clone.clone.1 | custom fusion | bytes 1052672 | tf_op jit(solution)/shard_map/while/body/eval_jaxpr/jit(_take)/gather | solution.py:44
  156.5 3.9 %gather_fusion.3 = bf16[1024,256]{1,0:T(8,128)(2,1)S(1)} fusion(bf16[256,64]{0,1:T(8,128)(2,1)S(1)} %get-tuple-element.464, s32[1024]{0:T(1024)S(1)} %get-tuple-element.404), kind=kCustom, calls=%fused_computation.3.clone.clone.1 | custom fusion | bytes 1052672 | tf_op jit(solution)/shard_map/while/body/eval_jaxpr/jit(_take)/gather | solution.py:43
  (87 shorter events, 18.3 us)
Async XLA Ops:
  6.8 0.8 copy-start.1
  18.0 0.8 copy-start.1
  29.2 0.8 copy-start.1
  40.4 8.7 %copy-start.9 = (s32[5]{0:T(128)S(1)}, s32[5]{0:T(128)}, u32[]{:S(2)}) copy-start(s32[5]{0:T(128)} %param.25) | copy-start | bytes 64
  40.4 8.8 %copy-start.8 = (bf16[5,64]{1,0:T(8,128)(2,1)S(1)}, bf16[5,64]{1,0:T(8,128)(2,1)}, u32[]{:S(2)}) copy-start(bf16[5,64]{1,0:T(8,128)(2,1)} %param.24) | copy-start | bytes 1924
  40.5 32.8 %copy-start.7 = (s32[2080]{0:T(1024)S(1)}, s32[2080]{0:T(1024)}, u32[]{:S(2)}) copy-start(s32[2080]{0:T(1024)} %constant.170) | copy-start | bytes 24964
  40.9 37.1 %copy-start.6 = (s32[2080]{0:T(1024)S(1)}, s32[2080]{0:T(1024)}, u32[]{:S(2)}) copy-start(s32[2080]{0:T(1024)} %constant.171) | copy-start | bytes 24964
  41.7 41.1 %copy-start.11 = (u32[32]{0:T(128)S(1)}, u32[32]{0:T(128)}, u32[]{:S(2)}) copy-start(u32[32]{0:T(128)} %constant.174) | copy-start | bytes 388
  41.7 42.5 %all-to-all-start = ((bf16[8,260,64]{1,2,0:T(8,128)(2,1)}), bf16[8,260,64]{1,2,0:T(8,128)(2,1)S(1)}, u32[]{:S(2)}, u32[]{:S(2)}) async-start(bf16[8,260,64]{1,2,0:T(8,128)(2,1)} %copy.26), calls=%async_computation | async-start | bytes 786432 | tf_op jit(solution)/shard_map/all_to_all | solution.py:143
  119.9 4.3 %copy-start.10 = (f32[2080]{0:T(1024)S(1)}, f32[2080]{0:T(1024)}, u32[]{:S(2)}) copy-start(f32[2080]{0:T(1024)} %constant.145) | copy-start | bytes 24964
  120.7 12.6 %all-to-all-start.1 = ((bf16[8,260,64]{1,2,0:T(8,128)(2,1)}), bf16[8,260,64]{1,2,0:T(8,128)(2,1)S(1)}, u32[]{:S(2)}, u32[]{:S(2)}) async-start(bf16[8,260,64]{1,2,0:T(8,128)(2,1)} %copy.28), calls=%async_computation.1 | async-start | bytes 786432 | tf_op jit(solution)/shard_map/all_to_all | solution.py:151
  128.0 5.8 %copy-start = (bf16[1,256,64]{1,2,0:T(8,128)(2,1)S(1)}, bf16[1,256,64]{1,2,0:T(8,128)(2,1)}, u32[]{:S(2)}) copy-start(bf16[1,256,64]{1,2,0:T(8,128)(2,1)} %param.19) | copy-start | bytes 98308
  128.0 5.8 %copy-start.3 = (s32[3072]{0:T(1024)S(1)}, s32[3072]{0:T(1024)}, u32[]{:S(2)}) copy-start(s32[3072]{0:T(1024)} %get-tuple-element.477) | copy-start | bytes 36868
  128.0 5.8 %copy-start.4 = (s32[3072]{0:T(1024)S(1)}, s32[3072]{0:T(1024)}, u32[]{:S(2)}) copy-start(s32[3072]{0:T(1024)} %get-tuple-element.478) | copy-start | bytes 36868
  133.9 27.9 %copy-start.2 = (bf16[256,64]{0,1:T(8,128)(2,1)S(1)}, bf16[256,64]{0,1:T(8,128)(2,1)}, u32[]{:S(2)}) copy-start(bf16[256,64]{0,1:T(8,128)(2,1)} %get-tuple-element.474) | copy-start | bytes 98308
  133.9 27.9 %copy-start.5 = (bf16[1,256,64]{1,2,0:T(8,128)(2,1)S(1)}, bf16[1,256,64]{1,2,0:T(8,128)(2,1)}, u32[]{:S(2)}) copy-start(bf16[1,256,64]{1,2,0:T(8,128)(2,1)} %param.21) | copy-start | bytes 98308
where the time goes:
time: 164 us; the launch traced here: 163 us
  local copies, waits for them, and re-layouts  69.6 us (42%)
  blocking collectives  59.3 us (36%)
  starting transfers between devices  10.9 us (7%)
  other arithmetic  8.08 us (5%)
  matrix products  7.18 us (4%)
  waiting for transfers between devices  5.25 us (3%)
  between operations  2.25 us (1%)
    all_gather x1, blocking collectives, on_device(): shard_portion = lax.all_gather(final_slice, 'wide', axis=0, tiled=True)  33.2 us
    gather x7, local copies, waits for them, and re-layouts, pair_block(): leading_columns = jnp.take(rows, lead_part, axis=1).astype(jnp.float32)  28.4 us
    gather x7, local copies, waits for them, and re-layouts, pair_block(): right_cols = jnp.take(rows, trail_part, axis=1).astype(jnp.float32)  28.4 us
    unnamed x2, blocking collectives  24.3 us
    all_to_all x1, starting transfers between devices, on_device(): lax.all_to_all(span_state.reshape(wide_count, rows_per, head_width), 'wid...  7.41 us
    all_to_all x1, waiting for transfers between devices, on_device(): lax.all_to_all(rounded[:wide_count], 'wide', split_axis=0, concat_axis=0,...  5.25 us
    unnamed x27, local copies, waits for them, and re-layouts  4.03 us
    all_to_all x1, starting transfers between devices, on_device(): lax.all_to_all(rounded[:wide_count], 'wide', split_axis=0, concat_axis=0,...  3.45 us
  transfers between devices with their start and end apart: 2, of which 1 were waited for; matrix products, arithmetic and copies ran while one was open for 7% of the time, Pallas kernels for 0%

commit v1 on v0

--- a/solution.py
+++ b/solution.py
@@ -162,7 +162,23 @@
     pair_rows = lax.all_gather(masked, "narrow", axis=1, tiled=True)
     own_rows = lax.dynamic_index_in_dim(pair_rows, prompt_lane, 0, keepdims=False)
     initial = jnp.zeros((own_rows.shape[0], head_width), jnp.float32)
-    shard_portion = lax.all_gather(final_slice, "wide", axis=0, tiled=True)
+    v1 = lax.axis_size("wide")
+    before, out_arr, work_now = (v1, lax.axis_index("wide"), final_slice.shape[0])
+    inbox = [p * before if j0 == 0 else p for j0, p in enumerate(final_slice.shape)]
+    shard_portion = lax.dynamic_update_slice_in_dim(
+        jnp.zeros(inbox, final_slice.dtype), final_slice, out_arr * work_now, axis=0
+    )
+    a_now = res = final_slice
+    for rr in range(1, before // 2 + 1):
+        a_now = lax.ppermute(a_now, "wide", [(j0, (j0 + 1) % before) for j0 in range(before)])
+        shard_portion = lax.dynamic_update_slice_in_dim(
+            shard_portion, a_now, (out_arr - rr) % before * work_now, axis=0
+        )
+        if 2 * rr < before:
+            res = lax.ppermute(res, "wide", [(j0, (j0 - 1) % before) for j0 in range(before)])
+            shard_portion = lax.dynamic_update_slice_in_dim(
+                shard_portion, res, (out_arr + rr) % before * work_now, axis=0
+            )
     piece_rows = shard_portion.shape[0]
     features = pair_block(
         own_rows,

time: 164 us -> 152 us (0.927)
  blocking collectives: 59.3 us -> 26.4 us
  starting transfers between devices: 10.9 us -> 28 us
  local copies, waits for them, and re-layouts: 69.6 us -> 74.1 us
    all_gather x1 -> x0, blocking collectives: 33.2 us -> none  [on_device(): shard_portion = lax.all_gather(final_slice, 'wide', axis=0, tiled=True)]
    ppermute x0 -> x7, starting transfers between devices: none -> 14.6 us  [the longest x3 13.6 us: on_device(): lax.ppermute(res, 'wide', [(j0, (j0 - 1) % before) for j0 in range(before)])]
    dynamic_update_slice x0 -> x8, local copies, waits for them, and re-layouts: none -> 5.39 us  [the longest x4 2.71 us: on_device(): lax.dynamic_update_slice_in_dim(shard_portion, a_now, (out_arr - rr) % be...]
    all_to_all x1, waiting for transfers between devices: 5.25 us -> 0.74 us  [on_device(): lax.all_to_all(rounded[:wide_count], 'wide', split_axis=0, concat_axis=0,...]
    ppermute x0 -> x7, waiting for transfers between devices: none -> 4.05 us  [the longest x4 2.48 us: on_device(): lax.ppermute(a_now, 'wide', [(j0, (j0 + 1) % before) for j0 in range(befo...]
    all_to_all x1, starting transfers between devices: 3.45 us -> 6.04 us  [on_device(): lax.all_to_all(rounded[:wide_count], 'wide', split_axis=0, concat_axis=0,...]
    unnamed x27 -> x28, local copies, waits for them, and re-layouts: 4.03 us -> 4.56 us
  transfers between devices with their start and end apart: 2 -> 9, of which waited for: 1 -> 5; matrix products, arithmetic and copies ran while one was open for 7% -> 12% of each run, Pallas kernels for 0% -> 0%
where the time goes in v1:
time: 152 us; the launch traced here: 151 us
  local copies, waits for them, and re-layouts  74.1 us (49%)
  starting transfers between devices  28 us (18%)
  blocking collectives  26.4 us (17%)
  other arithmetic  8.08 us (5%)
  matrix products  7.19 us (5%)
  waiting for transfers between devices  4.79 us (3%)
  between operations  2.41 us (2%)
    gather x7, local copies, waits for them, and re-layouts, pair_block(): leading_columns = jnp.take(rows, lead_part, axis=1).astype(jnp.float32)  28.4 us
    gather x7, local copies, waits for them, and re-layouts, pair_block(): right_cols = jnp.take(rows, trail_part, axis=1).astype(jnp.float32)  28.4 us
    unnamed x2, blocking collectives  24.5 us
    ppermute x3, starting transfers between devices, on_device(): lax.ppermute(res, 'wide', [(j0, (j0 - 1) % before) for j0 in range(before)])  13.6 us
    all_to_all x1, starting transfers between devices, on_device(): lax.all_to_all(span_state.reshape(wide_count, rows_per, head_width), 'wid...  7.28 us
    all_to_all x1, starting transfers between devices, on_device(): lax.all_to_all(rounded[:wide_count], 'wide', split_axis=0, concat_axis=0,...  6.04 us
    unnamed x28, local copies, waits for them, and re-layouts  4.56 us
    dot_general x3, matrix products, fill_block(): lax.dot_general(features, spread, (((0,), (0,)), ((), ())), preferred_ele...  3.39 us
  transfers between devices with their start and end apart: 9, of which 5 were waited for; matrix products, arithmetic and copies ran while one was open for 12% of the time, Pallas kernels for 0%

profile of v1, /device:TPU:0, one launch (start us, length us, event | category | flops | bytes accessed | tf_op | source)
XLA Modules:
  0.0 151.2 jit_solution(14769203663458236600)
XLA Ops:
  3.5 1.3 dynamic-slice
  4.8 1.3 slice_dynamic-update-slice_fusion
  6.9 33.6 %while.29 = (s32[]{:T(128)}, bf16[3072,64]{0,1:T(8,128)(2,1)S(1)}, bf16[256,64]{0,1:T(8,128)(2,1)}, bf16[256,64]{1,0:T(8,128)(2,1)S(1)}, s32[]{:T(128)}, /*index...) while((s32[]{:T(128)}, bf16[3072,64]{0,1:T(8,128)(2,1)S(1)}, ...), condition=%wide.region_4.6_spmd.clone, body=%wide.region_3.5_spmd.sunk.clone.sunk | while | flops 35475460 | bytes 3522759 | solution.py:68
  7.7 3.9 %gather_fusion = bf16[1024,256]{1,0:T(8,128)(2,1)S(1)} fusion(bf16[256,64]{0,1:T(8,128)(2,1)S(1)} %copy-done.1, s32[1024]{0:T(1024)S(1)} %get-tuple-element.395), kind=kCustom, calls=%fused_computation.2.clone.clone.1 | custom fusion | bytes 1052672 | tf_op jit(solution)/shard_map/while/body/eval_jaxpr/jit(_take)/gather | solution.py:44
  11.6 3.9 %gather_fusion.1 = bf16[1024,256]{1,0:T(8,128)(2,1)S(1)} fusion(bf16[256,64]{0,1:T(8,128)(2,1)S(1)} %copy-done.1, s32[1024]{0:T(1024)S(1)} %get-tuple-element.396), kind=kCustom, calls=%fused_computation.clone.clone.1 | custom fusion | bytes 1052672 | tf_op jit(solution)/shard_map/while/body/eval_jaxpr/jit(_take)/gather | solution.py:43
  17.0 1.1 fusion.87
  18.9 3.9 %gather_fusion = bf16[1024,256]{1,0:T(8,128)(2,1)S(1)} fusion(bf16[256,64]{0,1:T(8,128)(2,1)S(1)} %copy-done.1, s32[1024]{0:T(1024)S(1)} %get-tuple-element.395), kind=kCustom, calls=%fused_computation.2.clone.clone.1 | custom fusion | bytes 1052672 | tf_op jit(solution)/shard_map/while/body/eval_jaxpr/jit(_take)/gather | solution.py:44
  22.8 3.9 %gather_fusion.1 = bf16[1024,256]{1,0:T(8,128)(2,1)S(1)} fusion(bf16[256,64]{0,1:T(8,128)(2,1)S(1)} %copy-done.1, s32[1024]{0:T(1024)S(1)} %get-tuple-element.396), kind=kCustom, calls=%fused_computation.clone.clone.1 | custom fusion | bytes 1052672 | tf_op jit(solution)/shard_map/while/body/eval_jaxpr/jit(_take)/gather | solution.py:43
  28.2 1.1 fusion.87
  30.1 3.9 %gather_fusion = bf16[1024,256]{1,0:T(8,128)(2,1)S(1)} fusion(bf16[256,64]{0,1:T(8,128)(2,1)S(1)} %copy-done.1, s32[1024]{0:T(1024)S(1)} %get-tuple-element.395), kind=kCustom, calls=%fused_computation.2.clone.clone.1 | custom fusion | bytes 1052672 | tf_op jit(solution)/shard_map/while/body/eval_jaxpr/jit(_take)/gather | solution.py:44
  34.0 3.9 %gather_fusion.1 = bf16[1024,256]{1,0:T(8,128)(2,1)S(1)} fusion(bf16[256,64]{0,1:T(8,128)(2,1)S(1)} %copy-done.1, s32[1024]{0:T(1024)S(1)} %get-tuple-element.396), kind=kCustom, calls=%fused_computation.clone.clone.1 | custom fusion | bytes 1052672 | tf_op jit(solution)/shard_map/while/body/eval_jaxpr/jit(_take)/gather | solution.py:43
  39.4 1.1 fusion.87
  41.8 7.3 %all-to-all-start = ((bf16[8,260,64]{1,2,0:T(8,128)(2,1)}), bf16[8,260,64]{1,2,0:T(8,128)(2,1)S(1)}, u32[]{:S(2)}, u32[]{:S(2)}) async-start(bf16[8,260,64]{1,2,0:T(8,128)(2,1)} %copy.24), calls=%async_computation | async-start | bytes 786432 | tf_op jit(solution)/shard_map/all_to_all | solution.py:143
  49.1 22.1 %all-reduce.1 = f32[8]{0:T(128)S(1)} all-reduce(f32[8]{0:T(128)S(1)} %get-tuple-element.337), channel_id=1, replica_groups=mesh['groups'=2,'wide'=8,'narrow'=2] {'wide'}, use_global_device_ids=true, to_apply=%add.1 | all-reduce | flops 8 | bytes 64
  72.6 1.0 collective-permute-start
  73.7 3.8 %collective-permute-start.1 = (bf16[260,64]{0,1:T(8,128)(2,1)S(1)}, bf16[260,64]{0,1:T(8,128)(2,1)S(1)}, u32[]{:S(2)}, u32[]{:S(2)}) collective-permute-start(bf16[260,64]{0,1:T(8,128)(2,1)S(1)} %bitcast.94), channel_id=1, source_target_pairs={{0,14},{2,0},{4,2},{6,4},{8,6},{10,8},{12,10},{14,12},{1,15},{3,1}... | collective-permute-start | bytes 99848 | tf_op jit(solution)/shard_map/ppermute | solution.py:178
  77.5 2.1 %collective-permute-done = bf16[260,64]{0,1:T(8,128)(2,1)S(1)} collective-permute-done((bf16[260,64]{0,1:T(8,128)(2,1)S(1)}, bf16[260,64]{0,1:T(8,128)(2,1)S(1)}, u32[]{:S(2)}, u32[]{:S(2)}) %collective-permute-start) | collective-permute-done | bytes 33312 | tf_op jit(solution)/shard_map/ppermute | solution.py:173
  79.6 1.8 %all_gather.7 = bf16[2,10,64]{2,0,1:T(2,128)(2,1)S(1)} all-gather(bf16[2,5,64]{2,0,1:T(2,128)(2,1)S(1)} %broadcast_select_fusion), channel_id=1, replica_groups=mesh['groups'=2,'wide'=8,'narrow'=2] {'narrow'}, dimensions={1}, use_global_device_ids=true | all-gather | bytes 3840 | tf_op jit(solution)/shard_map/all_gather | solution.py:162
  81.5 4.8 %collective-permute-start.3 = (bf16[260,64]{0,1:T(8,128)(2,1)S(1)}, bf16[260,64]{0,1:T(8,128)(2,1)S(1)}, u32[]{:S(2)}, u32[]{:S(2)}) collective-permute-start(bf16[260,64]{0,1:T(8,128)(2,1)S(1)} %collective-permute-done.1), channel_id=1, source_target_pairs={{0,14},{2,0},{4,2},{6,4},{8,6},{10,8},{12,10},{14,12},{1,15},{3,1}... | collective-permute-start | bytes 99848 | tf_op jit(solution)/shard_map/ppermute | solution.py:178
  86.4 1.6 %collective-permute-done.3 = bf16[260,64]{0,1:T(8,128)(2,1)S(1)} collective-permute-done((bf16[260,64]{0,1:T(8,128)(2,1)S(1)}, bf16[260,64]{0,1:T(8,128)(2,1)S(1)}, u32[]{:S(2)}, u32[]{:S(2)}) %collective-permute-start.3) | collective-permute-done | bytes 33312 | tf_op jit(solution)/shard_map/ppermute | solution.py:178
  88.0 5.0 %collective-permute-start.5 = (bf16[260,64]{0,1:T(8,128)(2,1)S(1)}, bf16[260,64]{0,1:T(8,128)(2,1)S(1)}, u32[]{:S(2)}, u32[]{:S(2)}) collective-permute-start(bf16[260,64]{0,1:T(8,128)(2,1)S(1)} %collective-permute-done.3), channel_id=1, source_target_pairs={{0,14},{2,0},{4,2},{6,4},{8,6},{10,8},{12,10},{14,12},{1,15},{3,1}... | collective-permute-start | bytes 99848 | tf_op jit(solution)/shard_map/ppermute | solution.py:178
  93.4 4.8 %gather_fusion.4 = bf16[2080,10]{1,0:T(8,128)(2,1)S(1)} fusion(bf16[10,64]{0,1:T(8,128)(2,1)S(1)} %bitcast.91, s32[3072]{0:T(1024)S(1)} %pad_clamp_fusion.1), kind=kCustom, calls=%fused_computation.1.clone | custom fusion | bytes 91520 | tf_op jit(solution)/shard_map/jit(_take)/gather | solution.py:43
  98.2 4.8 %gather_fusion.5 = bf16[2080,10]{1,0:T(8,128)(2,1)S(1)} fusion(bf16[10,64]{0,1:T(8,128)(2,1)S(1)} %bitcast.92, s32[3072]{0:T(1024)S(1)} %pad_clamp_fusion), kind=kCustom, calls=%fused_computation.5.clone | custom fusion | bytes 91520 | tf_op jit(solution)/shard_map/jit(_take)/gather | solution.py:44
  105.1 6.0 %all-to-all-start.1 = ((bf16[8,260,64]{1,2,0:T(8,128)(2,1)}), bf16[8,260,64]{1,2,0:T(8,128)(2,1)S(1)}, u32[]{:S(2)}, u32[]{:S(2)}) async-start(bf16[8,260,64]{1,2,0:T(8,128)(2,1)} %copy.26), calls=%async_computation.1 | async-start | bytes 786432 | tf_op jit(solution)/shard_map/all_to_all | solution.py:151
  117.2 2.5 %all-reduce.2 = f32[10,64]{1,0:T(8,128)S(1)} all-reduce(f32[10,64]{1,0:T(8,128)S(1)} %fusion.42), channel_id=2, replica_groups=mesh['groups'=2,'wide'=8,'narrow'=2] {'narrow'}, use_global_device_ids=true, to_apply=%region_8.11.clone | all-reduce | flops 640 | bytes 5120
  122.2 27.9 %while.30 = (s32[]{:T(128)}, f32[256,64]{0,1:T(8,128)S(1)}, bf16[256,64]{0,1:T(8,128)(2,1)S(1)}, bf16[3072,64]{0,1:T(8,128)(2,1)S(1)}, s32[]{:T(128)}, /*index=5...) while((s32[]{:T(128)}, f32[256,64]{0,1:T(8,128)S(1)}, ...), condition=%wide.region_6.8_spmd.clone.clone, body=%wide.region_5.7_spmd.sunk.clone.clone.sunk | while | flops 35442696 | bytes 3457205 | solution.py:88
  122.3 3.9 %gather_fusion.2 = bf16[1024,256]{1,0:T(8,128)(2,1)S(1)} fusion(bf16[256,64]{0,1:T(8,128)(2,1)S(1)} %get-tuple-element.464, s32[1024]{0:T(1024)S(1)} %get-tuple-element.403), kind=kCustom, calls=%fused_computation.4.clone.clone.1 | custom fusion | bytes 1052672 | tf_op jit(solution)/shard_map/while/body/eval_jaxpr/jit(_take)/gather | solution.py:44
  126.2 3.9 %gather_fusion.3 = bf16[1024,256]{1,0:T(8,128)(2,1)S(1)} fusion(bf16[256,64]{0,1:T(8,128)(2,1)S(1)} %get-tuple-element.464, s32[1024]{0:T(1024)S(1)} %get-tuple-element.404), kind=kCustom, calls=%fused_computation.3.clone.clone.1 | custom fusion | bytes 1052672 | tf_op jit(solution)/shard_map/while/body/eval_jaxpr/jit(_take)/gather | solution.py:43
  131.6 3.9 %gather_fusion.2 = bf16[1024,256]{1,0:T(8,128)(2,1)S(1)} fusion(bf16[256,64]{0,1:T(8,128)(2,1)S(1)} %get-tuple-element.464, s32[1024]{0:T(1024)S(1)} %get-tuple-element.403), kind=kCustom, calls=%fused_computation.4.clone.clone.1 | custom fusion | bytes 1052672 | tf_op jit(solution)/shard_map/while/body/eval_jaxpr/jit(_take)/gather | solution.py:44
  135.5 3.9 %gather_fusion.3 = bf16[1024,256]{1,0:T(8,128)(2,1)S(1)} fusion(bf16[256,64]{0,1:T(8,128)(2,1)S(1)} %get-tuple-element.464, s32[1024]{0:T(1024)S(1)} %get-tuple-element.404), kind=kCustom, calls=%fused_computation.3.clone.clone.1 | custom fusion | bytes 1052672 | tf_op jit(solution)/shard_map/while/body/eval_jaxpr/jit(_take)/gather | solution.py:43
  140.9 3.9 %gather_fusion.2 = bf16[1024,256]{1,0:T(8,128)(2,1)S(1)} fusion(bf16[256,64]{0,1:T(8,128)(2,1)S(1)} %get-tuple-element.464, s32[1024]{0:T(1024)S(1)} %get-tuple-element.403), kind=kCustom, calls=%fused_computation.4.clone.clone.1 | custom fusion | bytes 1052672 | tf_op jit(solution)/shard_map/while/body/eval_jaxpr/jit(_take)/gather | solution.py:44
  144.8 3.9 %gather_fusion.3 = bf16[1024,256]{1,0:T(8,128)(2,1)S(1)} fusion(bf16[256,64]{0,1:T(8,128)(2,1)S(1)} %get-tuple-element.464, s32[1024]{0:T(1024)S(1)} %get-tuple-element.404), kind=kCustom, calls=%fused_computation.3.clone.clone.1 | custom fusion | bytes 1052672 | tf_op jit(solution)/shard_map/while/body/eval_jaxpr/jit(_take)/gather | solution.py:43
  (108 shorter events, 27.6 us)
Async XLA Ops:
  6.9 0.8 copy-start.1
  18.1 0.8 copy-start.1
  29.3 0.8 copy-start.1
  41.0 30.4 %copy-start.9 = (s32[5]{0:T(128)S(1)}, s32[5]{0:T(128)}, u32[]{:S(2)}) copy-start(s32[5]{0:T(128)} %param.25) | copy-start | bytes 64
  41.0 30.5 %copy-start.8 = (bf16[5,64]{1,0:T(8,128)(2,1)S(1)}, bf16[5,64]{1,0:T(8,128)(2,1)}, u32[]{:S(2)}) copy-start(bf16[5,64]{1,0:T(8,128)(2,1)} %param.24) | copy-start | bytes 1924
  41.8 29.8 %all-to-all-start = ((bf16[8,260,64]{1,2,0:T(8,128)(2,1)}), bf16[8,260,64]{1,2,0:T(8,128)(2,1)S(1)}, u32[]{:S(2)}, u32[]{:S(2)}) async-start(bf16[8,260,64]{1,2,0:T(8,128)(2,1)} %copy.24), calls=%async_computation | async-start | bytes 786432 | tf_op jit(solution)/shard_map/all_to_all | solution.py:143
  49.1 24.5 %copy-start.7 = (s32[2080]{0:T(1024)S(1)}, s32[2080]{0:T(1024)}, u32[]{:S(2)}) copy-start(s32[2080]{0:T(1024)} %constant.225) | copy-start | bytes 24964
  49.1 30.5 %copy-start.6 = (s32[2080]{0:T(1024)S(1)}, s32[2080]{0:T(1024)}, u32[]{:S(2)}) copy-start(s32[2080]{0:T(1024)} %constant.226) | copy-start | bytes 24964
  72.6 7.0 %collective-permute-start = (bf16[260,64]{0,1:T(8,128)(2,1)S(1)}, bf16[260,64]{0,1:T(8,128)(2,1)S(1)}, u32[]{:S(2)}, u32[]{:S(2)}) collective-permute-start(bf16[260,64]{0,1:T(8,128)(2,1)S(1)} %bitcast.93), channel_id=1, source_target_pairs={{0,2},{2,4},{4,6},{6,8},{8,10},{10,12},{12,14},{14,0},{1,3},{3,5},... | collective-permute-start | bytes 99848 | tf_op jit(solution)/shard_map/ppermute | solution.py:173
  73.7 7.8 %collective-permute-start.1 = (bf16[260,64]{0,1:T(8,128)(2,1)S(1)}, bf16[260,64]{0,1:T(8,128)(2,1)S(1)}, u32[]{:S(2)}, u32[]{:S(2)}) collective-permute-start(bf16[260,64]{0,1:T(8,128)(2,1)S(1)} %bitcast.94), channel_id=1, source_target_pairs={{0,14},{2,0},{4,2},{6,4},{8,6},{10,8},{12,10},{14,12},{1,15},{3,1}... | collective-permute-start | bytes 99848 | tf_op jit(solution)/shard_map/ppermute | solution.py:178
  79.6 6.8 %collective-permute-start.2 = (bf16[260,64]{0,1:T(8,128)(2,1)S(1)}, bf16[260,64]{0,1:T(8,128)(2,1)S(1)}, u32[]{:S(2)}, u32[]{:S(2)}) collective-permute-start(bf16[260,64]{0,1:T(8,128)(2,1)S(1)} %collective-permute-done), channel_id=1, source_target_pairs={{0,2},{2,4},{4,6},{6,8},{8,10},{10,12},{12,14},{14,0},{1,3},{3,5},... | collective-permute-start | bytes 99848 | tf_op jit(solution)/shard_map/ppermute | solution.py:173
  81.5 21.5 %copy-start.11 = (u32[32]{0:T(128)S(1)}, u32[32]{0:T(128)}, u32[]{:S(2)}) copy-start(u32[32]{0:T(128)} %constant.229) | copy-start | bytes 388
  81.5 6.5 %collective-permute-start.3 = (bf16[260,64]{0,1:T(8,128)(2,1)S(1)}, bf16[260,64]{0,1:T(8,128)(2,1)S(1)}, u32[]{:S(2)}, u32[]{:S(2)}) collective-permute-start(bf16[260,64]{0,1:T(8,128)(2,1)S(1)} %collective-permute-done.1), channel_id=1, source_target_pairs={{0,14},{2,0},{4,2},{6,4},{8,6},{10,8},{12,10},{14,12},{1,15},{3,1}... | collective-permute-start | bytes 99848 | tf_op jit(solution)/shard_map/ppermute | solution.py:178
  86.4 6.8 %collective-permute-start.4 = (bf16[260,64]{0,1:T(8,128)(2,1)S(1)}, bf16[260,64]{0,1:T(8,128)(2,1)S(1)}, u32[]{:S(2)}, u32[]{:S(2)}) collective-permute-start(bf16[260,64]{0,1:T(8,128)(2,1)S(1)} %collective-permute-done.2), channel_id=1, source_target_pairs={{0,2},{2,4},{4,6},{6,8},{8,10},{10,12},{12,14},{14,0},{1,3},{3,5},... | collective-permute-start | bytes 99848 | tf_op jit(solution)/shard_map/ppermute | solution.py:173
  88.0 27.1 %collective-permute-start.5 = (bf16[260,64]{0,1:T(8,128)(2,1)S(1)}, bf16[260,64]{0,1:T(8,128)(2,1)S(1)}, u32[]{:S(2)}, u32[]{:S(2)}) collective-permute-start(bf16[260,64]{0,1:T(8,128)(2,1)S(1)} %collective-permute-done.3), channel_id=1, source_target_pairs={{0,14},{2,0},{4,2},{6,4},{8,6},{10,8},{12,10},{14,12},{1,15},{3,1}... | collective-permute-start | bytes 99848 | tf_op jit(solution)/shard_map/ppermute | solution.py:178
  93.2 22.7 %collective-permute-start.6 = (bf16[260,64]{0,1:T(8,128)(2,1)S(1)}, bf16[260,64]{0,1:T(8,128)(2,1)S(1)}, u32[]{:S(2)}, u32[]{:S(2)}) collective-permute-start(bf16[260,64]{0,1:T(8,128)(2,1)S(1)} %collective-permute-done.4), channel_id=1, source_target_pairs={{0,2},{2,4},{4,6},{6,8},{8,10},{10,12},{12,14},{14,0},{1,3},{3,5},... | collective-permute-start | bytes 99848 | tf_op jit(solution)/shard_map/ppermute | solution.py:173
  105.1 11.5 %copy-start.10 = (f32[2080]{0:T(1024)S(1)}, f32[2080]{0:T(1024)}, u32[]{:S(2)}) copy-start(f32[2080]{0:T(1024)} %constant.200) | copy-start | bytes 24964
  105.1 16.2 %all-to-all-start.1 = ((bf16[8,260,64]{1,2,0:T(8,128)(2,1)}), bf16[8,260,64]{1,2,0:T(8,128)(2,1)S(1)}, u32[]{:S(2)}, u32[]{:S(2)}) async-start(bf16[8,260,64]{1,2,0:T(8,128)(2,1)} %copy.26), calls=%async_computation.1 | async-start | bytes 786432 | tf_op jit(solution)/shard_map/all_to_all | solution.py:151
  121.5 0.8 copy-start
  121.5 0.8 copy-start.3
  121.5 0.7 copy-start.4
  122.2 27.9 %copy-start.2 = (bf16[256,64]{0,1:T(8,128)(2,1)S(1)}, bf16[256,64]{0,1:T(8,128)(2,1)}, u32[]{:S(2)}) copy-start(bf16[256,64]{0,1:T(8,128)(2,1)} %get-tuple-element.474) | copy-start | bytes 98308
  122.2 27.9 %copy-start.5 = (bf16[1,256,64]{1,2,0:T(8,128)(2,1)S(1)}, bf16[1,256,64]{1,2,0:T(8,128)(2,1)}, u32[]{:S(2)}) copy-start(bf16[1,256,64]{1,2,0:T(8,128)(2,1)} %param.21) | copy-start | bytes 98308
